TPU v7x, 32 devices: a whole 2x2x4 slice. The times are simulated.
32 devices in a mesh: section: 4 (over y, x), expert: 8 (over z, core).
Axes of the slice: x: 2, y: 2, z: 4, core: 2. Of those that a mesh axis runs over, the one named last changes fastest.
Arguments:
- section_inputs: float32 [4, 1024, 2048], P('section', 'expert'), may hold values from -6 to 6
- stored_inputs: float32 [4, 1024, 2048], P('section', 'expert'), may hold values from -6 to 6
- out_grads: bfloat16 [4, 1024, 2048], P('section', 'expert'), may hold values from -6 to 6
- fwd_routes: int32 [4, 1024, 2], P('section', 'expert'), may hold values from 0 to 3, all different within a row; in each aligned block of 128 rows (0 to 127, 128 to 255, ..., all dimensions but the last counted through in order) at most 80 rows name the same one
- fwd_gates: float32 [4, 1024, 2], P('section', 'expert'), may hold values from 0.2 to 1
- fwd_modulation: float32 [4, 3, 2048], P('section'), may hold values from -3 to 3
- bwd_routes: int32 [4, 1024, 2], P('section', 'expert'), may hold values from 0 to 3, all different within a row; in each aligned block of 128 rows (0 to 127, 128 to 255, ..., all dimensions but the last counted through in order) at most 80 rows name the same one
- bwd_gates: float32 [4, 1024, 2], P('section', 'expert'), may hold values from 0.2 to 1
- bwd_modulation: float32 [4, 3, 2048], P('section'), may hold values from -3 to 3
- up_weight: bfloat16 [4, 8, 2048, 1024], P('section', 'expert'), may hold values from -0.125 to 0.125
- down_weight: bfloat16 [4, 8, 1024, 2048], P('section', 'expert'), may hold values from -0.125 to 0.125
Outputs:
- next_inputs: float32 [4, 1024, 2048], P('section', 'expert')
- input_grads: bfloat16 [4, 1024, 2048], P('section', 'expert')
Inputs may be any that keep to these rules, and one draw needn't show every extreme that they name: `fwd_routes`: A token names two different experts. In the rows of one index of expert (aligned blocks of 128 rows of a section) no expert is named more than 80 times, a bound that some block reaches. `bwd_routes`: A token names two different experts. In the rows of one index of expert (aligned blocks of 128 rows of a section) no expert is named more than 80 times, a bound that some block reaches.
All inputs are finite; a program needn't handle non-finite values.
Results may differ from a plain program's by a relative error of at most 0.0042.
Values may be sent and summed in bfloat16 or wider, within the bound.
A program may use at most 128 MiB of HBM per device.

v0:
```python
import jax
import jax.numpy as jnp
from jax import lax
from jax.sharding import PartitionSpec as P

norm_eps = 1e-06


def from_partner(array, axis, stride):
    return lax.ppermute(array, axis, [(i, i ^ 1 << stride) for i in range(lax.axis_size(axis))])


def from_behind(value, axis, steps):
    count = lax.axis_size(axis)
    leading, last = (max(0, -steps), min(count, count - steps))
    return lax.ppermute(value, axis, [(source, source + steps) for source in range(leading, last)])


def layer_norm(tok_rows):
    mean_row = jnp.mean(tok_rows, axis=-1, keepdims=True)
    centered = tok_rows - mean_row
    variance = jnp.mean(centered * centered, axis=-1, keepdims=True)
    inv_std = lax.rsqrt(variance + norm_eps)
    return (centered * inv_std, inv_std)


def slot_positions(routes, experts, capacity):
    flat_ids = routes.reshape(-1)
    choose = (flat_ids[:, None] == jnp.arange(experts, dtype=jnp.int32)[None, :]).astype(jnp.int32)
    before = jnp.cumsum(choose, axis=0) - choose
    slot_index = jnp.sum(before * choose, axis=1)
    return flat_ids * capacity + slot_index


def pack_slots(positions, pair_values, total_slots):
    selector = (positions[:, None] == jnp.arange(total_slots, dtype=jnp.int32)[None, :]).astype(
        jnp.bfloat16
    )
    return jnp.einsum(
        "ps,pd->sd", selector, pair_values, preferred_element_type=jnp.float32
    ).astype(jnp.bfloat16)


def expert_forward(slot_rows, up_block, down_block):
    width = slot_rows.shape[-1]
    flat_rows = slot_rows.reshape(-1, width)
    pre_act = jnp.dot(flat_rows, up_block, preferred_element_type=jnp.float32)
    activation = jax.nn.gelu(pre_act).astype(jnp.bfloat16)
    partial_value = jnp.dot(activation, down_block, preferred_element_type=jnp.float32).astype(
        jnp.bfloat16
    )
    return partial_value.reshape(slot_rows.shape)


def expert_backward(slot_rows, slot_grads, up_block, down_block):
    width = slot_rows.shape[-1]
    flat_rows = slot_rows.reshape(-1, width)
    flat_grads = slot_grads.reshape(-1, width)
    pre_act = jnp.dot(flat_rows, up_block, preferred_element_type=jnp.float32)
    act_grad = jnp.einsum("rd,fd->rf", flat_grads, down_block, preferred_element_type=jnp.float32)
    pre_grad = jax.vjp(jax.nn.gelu, pre_act)[1](act_grad)[0].astype(jnp.bfloat16)
    partial_value = jnp.einsum(
        "rf,df->rd", pre_grad, up_block, preferred_element_type=jnp.float32
    ).astype(jnp.bfloat16)
    return partial_value.reshape(slot_rows.shape)


def join_partner(own, other, parity):
    first = jnp.concatenate([own, other], axis=1)
    second = jnp.concatenate([other, own], axis=1)
    return jnp.where(parity == 0, first, second)


def add_halves(returned, experts, capacity, width):
    halves = returned.reshape(experts, 2, capacity, width).astype(jnp.float32)
    return (halves[:, 0] + halves[:, 1]).reshape(experts * capacity, width)


def forward_experts(send, up_block, down_block):
    units = lax.axis_size("expert")
    experts, capacity, width = send.shape
    half_slots = capacity // 2
    parity = lax.axis_index("expert") % 2
    own = lax.all_to_all(
        send.reshape(units, half_slots, width), "expert", split_axis=0, concat_axis=0, tiled=True
    )
    other = from_partner(own, "expert", 0)
    partial_value = expert_forward(join_partner(own, other, parity), up_block, down_block)
    returned = lax.all_to_all(partial_value, "expert", split_axis=0, concat_axis=0, tiled=True)
    return add_halves(returned, experts, capacity, width)


def backward_experts(send_rows, send_grads, up_block, down_block):
    units = lax.axis_size("expert")
    experts, capacity, width = send_rows.shape
    half_slots = capacity // 2
    parity = lax.axis_index("expert") % 2
    own_rows, own_grads = (
        lax.all_to_all(
            send_rows.reshape(units, half_slots, width),
            "expert",
            split_axis=0,
            concat_axis=0,
            tiled=True,
        ),
        lax.all_to_all(
            send_grads.reshape(units, half_slots, width),
            "expert",
            split_axis=0,
            concat_axis=0,
            tiled=True,
        ),
    )
    other_rows, other_grads = from_partner((own_rows, own_grads), "expert", 0)
    partial_value = expert_backward(
        join_partner(own_rows, other_rows, parity),
        join_partner(own_grads, other_grads, parity),
        up_block,
        down_block,
    )
    returned = lax.all_to_all(partial_value, "expert", split_axis=0, concat_axis=0, tiled=True)
    return add_halves(returned, experts, capacity, width)


def on_device(
    section_inputs,
    stored_inputs,
    out_grads,
    fwd_routes,
    fwd_gates,
    fwd_modulation,
    bwd_routes,
    bwd_gates,
    bwd_modulation,
    up_weight,
    down_weight,
):
    experts = lax.axis_size("expert") // 2
    tok_count = section_inputs.shape[1]
    width = section_inputs.shape[2]
    capacity = min(tok_count, 5 * tok_count // (2 * experts))
    total_slots = experts * capacity
    up_block = up_weight[0, 0]
    down_block = down_weight[0, 0]
    inputs = section_inputs[0]
    fwd_mod = fwd_modulation[0]
    normed, _ = layer_norm(inputs)
    hidden = (normed * (1.0 + fwd_mod[1]) + fwd_mod[0]).astype(jnp.bfloat16)
    positions = slot_positions(fwd_routes[0], experts, capacity)
    send = pack_slots(positions, jnp.repeat(hidden, 2, axis=0), total_slots).reshape(
        experts, capacity, width
    )
    results = forward_experts(send, up_block, down_block)
    pair_out = jnp.take(results, positions, axis=0).reshape(tok_count, 2, width)
    moe_out = jnp.sum(pair_out * fwd_gates[0][:, :, None], axis=1)
    out_fwd = inputs + fwd_mod[2] * moe_out
    next_inputs = from_behind(out_fwd[None], "section", 1)
    stored = stored_inputs[0]
    bwd_mod = bwd_modulation[0]
    normed_b, inv_b = layer_norm(stored)
    hidden_b = (normed_b * (1.0 + bwd_mod[1]) + bwd_mod[0]).astype(jnp.bfloat16)
    grad_rows = out_grads[0].astype(jnp.float32)
    pair_grads = (
        (bwd_gates[0][:, :, None] * (bwd_mod[2] * grad_rows)[:, None, :])
        .astype(jnp.bfloat16)
        .reshape(2 * tok_count, width)
    )
    positions_b = slot_positions(bwd_routes[0], experts, capacity)
    send_rows = pack_slots(positions_b, jnp.repeat(hidden_b, 2, axis=0), total_slots).reshape(
        experts, capacity, width
    )
    send_grads = pack_slots(positions_b, pair_grads, total_slots).reshape(experts, capacity, width)
    results_b = backward_experts(send_rows, send_grads, up_block, down_block)
    dhidden = jnp.sum(jnp.take(results_b, positions_b, axis=0).reshape(tok_count, 2, width), axis=1)
    dnorm = dhidden * (1.0 + bwd_mod[1])
    mean_one = jnp.mean(dnorm, axis=-1, keepdims=True)
    mean_two = jnp.mean(dnorm * normed_b, axis=-1, keepdims=True)
    section_grad = (grad_rows + (dnorm - mean_one - normed_b * mean_two) * inv_b).astype(
        jnp.bfloat16
    )
    input_grads = from_behind(section_grad[None], "section", -1)
    return (next_inputs, input_grads)


def solution(mesh):
    placed = (
        P("section", "expert", None),
        P("section", "expert", None),
        P("section", "expert", None),
        P("section", "expert", None),
        P("section", "expert", None),
        P("section", None, None),
        P("section", "expert", None),
        P("section", "expert", None),
        P("section", None, None),
        P("section", "expert", None, None),
        P("section", "expert", None, None),
    )
    return jax.shard_map(
        on_device,
        mesh=mesh,
        in_specs=placed,
        out_specs=(P("section", "expert", None), P("section", "expert", None)),
        check_vma=False,
    )
```

profile of v0, /device:TPU:0, one launch (start us, length us, event | category | flops | bytes accessed | tf_op | source)
XLA Modules:
  0.0 332.1 jit_solution(3101702258089992832)
XLA Ops:
  0.6 0.9 copy.22
  1.8 1.2 reduce-window.14
  3.5 0.7 fusion.68
  4.2 1.4 reduce_sum.95
  5.6 1.5 multiply_reduce_fusion.3
  7.3 0.6 broadcast_in_dim.13
  8.0 0.4 reshape.325
  8.4 1.7 convolution_convert_fusion.2
  10.2 6.4 %all-to-all-start = ((bf16[8,40,2048]{2,1,0:T(8,128)(2,1)}), bf16[8,40,2048]{2,1,0:T(8,128)(2,1)}, u32[]{:S(2)}, u32[]{:S(2)}) async-start(bf16[8,40,2048]{2,1,0:T(8,128)(2,1)} %bitcast.6), calls=%async_computation | async-start | bytes 2621440 | tf_op jit(solution)/shard_map/all_to_all | solution.py:84
  16.9 1.2 reduce-window.16
  18.6 2.5 mul.235
  21.2 2.7 mul.236
  24.2 1.7 convolution_convert_fusion.1
  25.9 22.8 %all-to-all-done = bf16[8,40,2048]{2,1,0:T(8,128)(2,1)} async-done(((bf16[8,40,2048]{2,1,0:T(8,128)(2,1)}), bf16[8,40,2048]{2,1,0:T(8,128)(2,1)}, u32[]{:S(2)}, u32[]{:S(2)}) %all-to-all-start) | async-done | bytes 1310752 | tf_op jit(solution)/shard_map/all_to_all | solution.py:84
  48.8 3.6 %all-to-all-start.2 = ((bf16[8,40,2048]{2,1,0:T(8,128)(2,1)}), bf16[8,40,2048]{2,1,0:T(8,128)(2,1)S(1)}, u32[]{:S(2)}, u32[]{:S(2)}) async-start(bf16[8,40,2048]{2,1,0:T(8,128)(2,1)} %bitcast.141), calls=%async_computation.2 | async-start | bytes 2621440 | tf_op jit(solution)/shard_map/all_to_all | solution.py:106
  53.0 0.6 broadcast_in_dim.14
  53.7 1.2 reshape.329
  54.9 2.9 convolution_convert_fusion
  57.9 26.6 %all-to-all-done.2 = bf16[8,40,2048]{2,1,0:T(8,128)(2,1)S(1)} async-done(((bf16[8,40,2048]{2,1,0:T(8,128)(2,1)}), bf16[8,40,2048]{2,1,0:T(8,128)(2,1)S(1)}, u32[]{:S(2)}, u32[]{:S(2)}) %all-to-all-start.2) | async-done | bytes 1310752 | tf_op jit(solution)/shard_map/all_to_all | solution.py:106
  84.5 3.8 %all-to-all-start.3 = ((bf16[8,40,2048]{2,1,0:T(8,128)(2,1)}), bf16[8,40,2048]{2,1,0:T(8,128)(2,1)S(1)}, u32[]{:S(2)}, u32[]{:S(2)}) async-start(bf16[8,40,2048]{2,1,0:T(8,128)(2,1)} %bitcast.25), calls=%async_computation.3 | async-start | bytes 2621440 | tf_op jit(solution)/shard_map/all_to_all | solution.py:99
  88.8 31.3 %all-to-all-done.3 = bf16[8,40,2048]{2,1,0:T(8,128)(2,1)S(1)} async-done(((bf16[8,40,2048]{2,1,0:T(8,128)(2,1)}), bf16[8,40,2048]{2,1,0:T(8,128)(2,1)S(1)}, u32[]{:S(2)}, u32[]{:S(2)}) %all-to-all-start.3) | async-done | bytes 1310752 | tf_op jit(solution)/shard_map/all_to_all | solution.py:99
  120.2 6.8 %maximum_select_fusion = (bf16[8,80,2048]{2,1,0:T(8,128)(2,1)}, bf16[8,80,2048]{2,1,0:T(8,128)(2,1)S(1)}) fusion(bf16[8,40,2048]{2,1,0:T(8,128)(2,1)} %collective-permute-done, bf16[8,40,2048]{2,1,0:T(8,128)(2,1)} %all-to-all-done, pred[]{:T(512)S(6)} %eq.87, bf16[8,40,2048]{2,1,0:T(8,128)(2,1)S(1)} %all-to-all-done.2, ...), kind=kLoop, calls=%fused_computation.41 | loop fusion | flops 23592960 | bytes 10485761 | tf_op jit(solution)/shard_map/jit(_where)/select_n | solution.py:71
  127.0 4.4 %fusion = f32[640,1024]{1,0:T(8,128)} fusion(bf16[640,2048]{1,0:T(8,128)(2,1)S(1)} %bitcast.146, bf16[1,1,1024,2048]{3,2,1,0:T(8,128)(2,1)S(1)} %copy-done.13), kind=kOutput, calls=%fused_computation.2 | convolution fusion | flops 2684354560 | bytes 9437184 | tf_op jit(solution)/shard_map/rd,fd->rf/dot_general | solution.py:60
  131.5 3.7 %maximum_select_fusion.2 = bf16[8,80,2048]{2,1,0:T(8,128)(2,1)} fusion(bf16[8,40,2048]{2,1,0:T(8,128)(2,1)} %collective-permute-done.3, bf16[8,40,2048]{2,1,0:T(8,128)(2,1)S(1)} %all-to-all-done.3, pred[]{:T(512)S(6)} %eq.87), kind=kLoop, calls=%fused_computation.43 | loop fusion | flops 11796480 | bytes 5242881 | tf_op jit(solution)/shard_map/jit(_where)/select_n | solution.py:71
  135.2 13.1 %fusion.10 = bf16[640,2048]{1,0:T(8,128)(2,1)} fusion(bf16[1,1,2048,1024]{3,2,1,0:T(8,128)(2,1)} %param.22, f32[640,1024]{1,0:T(8,128)} %fusion, bf16[640,2048]{1,0:T(8,128)(2,1)} %bitcast.144), kind=kOutput, calls=%fused_computation.15 | convolution fusion | flops 5383127040 | bytes 12058624 | tf_op jit(solution)/shard_map/rf,df->rd/dot_general | solution.py:62
  148.3 3.6 %all-to-all-start.4 = ((bf16[8,80,2048]{2,1,0:T(8,128)(2,1)}), bf16[8,80,2048]{2,1,0:T(8,128)(2,1)S(1)}, u32[]{:S(2)}, u32[]{:S(2)}) async-start(bf16[8,80,2048]{2,1,0:T(8,128)(2,1)} %bitcast.143), calls=%async_computation.4 | async-start | bytes 5242880 | tf_op jit(solution)/shard_map/all_to_all | solution.py:121
  151.9 11.7 %fusion.13 = bf16[640,2048]{1,0:T(8,128)(2,1)} fusion(bf16[1,1,1024,2048]{3,2,1,0:T(8,128)(2,1)} %param.23, bf16[640,2048]{1,0:T(8,128)(2,1)} %bitcast.145, bf16[1,1,2048,1024]{3,2,1,0:T(8,128)(2,1)} %param.22), kind=kOutput, calls=%fused_computation.16 | convolution fusion | flops 5375918080 | bytes 13631488 | tf_op jit(solution)/shard_map/dot_general | solution.py:49
  163.6 48.5 %all-to-all-done.4 = bf16[8,80,2048]{2,1,0:T(8,128)(2,1)S(1)} async-done(((bf16[8,80,2048]{2,1,0:T(8,128)(2,1)}), bf16[8,80,2048]{2,1,0:T(8,128)(2,1)S(1)}, u32[]{:S(2)}, u32[]{:S(2)}) %all-to-all-start.4) | async-done | bytes 2621472 | tf_op jit(solution)/shard_map/all_to_all | solution.py:121
  212.1 4.7 %all-to-all-start.1 = ((bf16[8,80,2048]{2,1,0:T(8,128)(2,1)}), bf16[8,80,2048]{2,1,0:T(8,128)(2,1)}, u32[]{:S(2)}, u32[]{:S(2)}) async-start(bf16[8,80,2048]{2,1,0:T(8,128)(2,1)} %bitcast.142), calls=%async_computation.1 | async-start | bytes 5242880 | tf_op jit(solution)/shard_map/all_to_all | solution.py:89
  217.0 0.7 convert.4
  217.7 0.4 fusion.31
  218.1 2.7 gather_fusion.1
  220.8 1.8 broadcast_select_fusion
  222.6 2.3 reshape.331
  224.9 4.2 %reduce_sum.102 = f32[128,2048]{1,0:T(8,128)S(1)} reduce(f32[128,2,2048]{2,1,0:T(2,128)} %reshape.331, f32[]{:T(128)} %constant.54.clone.1), dimensions={1}, to_apply=%region_11.13 | reduce | flops 262144 | bytes 3145732 | tf_op jit(solution)/shard_map/reduce_sum | solution.py:174
  229.4 47.5 %all-to-all-done.1 = bf16[8,80,2048]{2,1,0:T(8,128)(2,1)} async-done(((bf16[8,80,2048]{2,1,0:T(8,128)(2,1)}), bf16[8,80,2048]{2,1,0:T(8,128)(2,1)}, u32[]{:S(2)}, u32[]{:S(2)}) %all-to-all-start.1) | async-done | bytes 2621472 | tf_op jit(solution)/shard_map/all_to_all | solution.py:89
  276.9 2.4 convert.3
  279.3 0.4 fusion.32
  279.7 2.7 gather_fusion
  282.4 1.8 broadcast_select_fusion.1
  284.2 2.3 reshape.327
  286.5 5.0 %multiply_reduce_fusion = f32[128,2048]{1,0:T(8,128)S(1)} fusion(f32[128,2,2048]{2,1,0:T(2,128)} %reshape.327, f32[128,2]{1,0:T(8,128)S(1)} %copy.28), kind=kLoop, calls=%fused_computation.45 | loop fusion | flops 786432 | bytes 3146752 | tf_op jit(solution)/shard_map/reduce_sum | solution.py:155
  291.7 3.5 %collective-permute-start.1 = (f32[1,128,2048]{2,1,0:T(8,128)S(1)}, f32[1,128,2048]{2,1,0:T(8,128)S(1)}, u32[]{:S(2)}, u32[]{:S(2)}) collective-permute-start(f32[1,128,2048]{2,1,0:T(8,128)S(1)} %fusion.44), channel_id=1, source_target_pairs={{0,8},{8,16},{16,24},{1,9},{9,17},{17,25},{2,10},{10,18},{18,26},{... | collective-permute-start | bytes 3145736 | tf_op jit(solution)/shard_map/ppermute | solution.py:16
  295.2 0.7 fusion.39
  295.8 1.3 collective-permute-start.4
  297.1 33.2 %collective-permute-done.4 = bf16[1,128,2048]{2,1,0:T(8,128)(2,1)S(1)} collective-permute-done((bf16[1,128,2048]{2,1,0:T(8,128)(2,1)S(1)}, bf16[1,128,2048]{2,1,0:T(8,128)(2,1)S(1)}, u32[]{:S(2)}, u32[]{:S(2)}) %collective-permute-start.4) | collective-permute-done | bytes 524320 | tf_op jit(solution)/shard_map/ppermute | solution.py:16
  330.4 1.0 copy.46
  331.3 0.8 copy.47
  (79 shorter events, 4.0 us)
Async XLA Ops:
  0.6 6.4 %copy-start.3 = (f32[1,128,2048]{2,1,0:T(8,128)S(1)}, f32[1,128,2048]{2,1,0:T(8,128)}, u32[]{:S(2)}) copy-start(f32[1,128,2048]{2,1,0:T(8,128)} %param.13) | copy-start | bytes 3145732
  8.4 8.1 %copy-start.10 = (s32[1,128,2]{1,2,0:T(2,128)S(1)}, s32[1,128,2]{1,2,0:T(2,128)}, u32[]{:S(2)}) copy-start(s32[1,128,2]{1,2,0:T(2,128)} %param.19) | copy-start | bytes 3076
  8.4 10.1 %copy-start.9 = (f32[1,3,2048]{2,0,1:T(1,128)S(1)}, f32[1,3,2048]{2,0,1:T(1,128)}, u32[]{:S(2)}) copy-start(f32[1,3,2048]{2,0,1:T(1,128)} %param.21) | copy-start | bytes 73732
  8.4 10.1 %copy-start.7 = (bf16[1,128,2048]{2,1,0:T(8,128)(2,1)S(1)}, bf16[1,128,2048]{2,1,0:T(8,128)(2,1)}, u32[]{:S(2)}) copy-start(bf16[1,128,2048]{2,1,0:T(8,128)(2,1)} %param.15) | copy-start | bytes 1572868
  10.2 38.6 %all-to-all-start = ((bf16[8,40,2048]{2,1,0:T(8,128)(2,1)}), bf16[8,40,2048]{2,1,0:T(8,128)(2,1)}, u32[]{:S(2)}, u32[]{:S(2)}) async-start(bf16[8,40,2048]{2,1,0:T(8,128)(2,1)} %bitcast.6), calls=%async_computation | async-start | bytes 2621440 | tf_op jit(solution)/shard_map/all_to_all | solution.py:84
  21.2 2.7 copy-start.11
  24.2 28.1 %copy-start = (f32[1,128,2048]{2,1,0:T(8,128)S(1)}, f32[1,128,2048]{2,1,0:T(8,128)}, u32[]{:S(2)}) copy-start(f32[1,128,2048]{2,1,0:T(8,128)} %param.14) | copy-start | bytes 3145732
  48.8 35.7 %all-to-all-start.2 = ((bf16[8,40,2048]{2,1,0:T(8,128)(2,1)}), bf16[8,40,2048]{2,1,0:T(8,128)(2,1)S(1)}, u32[]{:S(2)}, u32[]{:S(2)}) async-start(bf16[8,40,2048]{2,1,0:T(8,128)(2,1)} %bitcast.141), calls=%async_computation.2 | async-start | bytes 2621440 | tf_op jit(solution)/shard_map/all_to_all | solution.py:106
  84.5 35.7 %all-to-all-start.3 = ((bf16[8,40,2048]{2,1,0:T(8,128)(2,1)}), bf16[8,40,2048]{2,1,0:T(8,128)(2,1)S(1)}, u32[]{:S(2)}, u32[]{:S(2)}) async-start(bf16[8,40,2048]{2,1,0:T(8,128)(2,1)} %bitcast.25), calls=%async_computation.3 | async-start | bytes 2621440 | tf_op jit(solution)/shard_map/all_to_all | solution.py:99
  88.2 31.9 %collective-permute-start = (bf16[8,40,2048]{2,1,0:T(8,128)(2,1)}, bf16[8,40,2048]{2,1,0:T(8,128)(2,1)}, u32[]{:S(2)}, u32[]{:S(2)}) collective-permute-start(bf16[8,40,2048]{2,1,0:T(8,128)(2,1)} %all-to-all-done), channel_id=1, source_target_pairs={{0,1},{1,0},{2,3},{3,2},{4,5},{5,4},{6,7},{7,6},{8,9},{9,8},{10,11... | collective-permute-start | bytes 3932168 | tf_op jit(solution)/shard_map/ppermute | solution.py:10
  88.5 31.7 %collective-permute-start.2 = (bf16[8,40,2048]{2,1,0:T(8,128)(2,1)S(1)}, bf16[8,40,2048]{2,1,0:T(8,128)(2,1)}, u32[]{:S(2)}, u32[]{:S(2)}) collective-permute-start(bf16[8,40,2048]{2,1,0:T(8,128)(2,1)S(1)} %all-to-all-done.2), channel_id=1, source_target_pairs={{0,1},{1,0},{2,3},{3,2},{4,5},{5,4},{6,7},{7,6},{8,9},{9,8},{10,11... | collective-permute-start | bytes 3932168 | tf_op jit(solution)/shard_map/ppermute | solution.py:10
  120.2 11.3 %collective-permute-start.3 = (bf16[8,40,2048]{2,1,0:T(8,128)(2,1)S(1)}, bf16[8,40,2048]{2,1,0:T(8,128)(2,1)}, u32[]{:S(2)}, u32[]{:S(2)}) collective-permute-start(bf16[8,40,2048]{2,1,0:T(8,128)(2,1)S(1)} %all-to-all-done.3), channel_id=1, source_target_pairs={{0,1},{1,0},{2,3},{3,2},{4,5},{5,4},{6,7},{7,6},{8,9},{9,8},{10,11... | collective-permute-start | bytes 3932168 | tf_op jit(solution)/shard_map/ppermute | solution.py:10
  120.2 6.9 %copy-start.13 = (bf16[1,1,1024,2048]{3,2,1,0:T(8,128)(2,1)S(1)}, bf16[1,1,1024,2048]{3,2,1,0:T(8,128)(2,1)}, u32[]{:S(2)}) copy-start(bf16[1,1,1024,2048]{3,2,1,0:T(8,128)(2,1)} %param.23) | copy-start | bytes 12582916
  148.3 63.8 %all-to-all-start.4 = ((bf16[8,80,2048]{2,1,0:T(8,128)(2,1)}), bf16[8,80,2048]{2,1,0:T(8,128)(2,1)S(1)}, u32[]{:S(2)}, u32[]{:S(2)}) async-start(bf16[8,80,2048]{2,1,0:T(8,128)(2,1)} %bitcast.143), calls=%async_computation.4 | async-start | bytes 5242880 | tf_op jit(solution)/shard_map/all_to_all | solution.py:121
  212.1 4.7 %copy-start.12 = (f32[1,128,2]{1,2,0:T(2,128)S(1)}, f32[1,128,2]{1,2,0:T(2,128)}, u32[]{:S(2)}) copy-start(f32[1,128,2]{1,2,0:T(2,128)} %param.17) | copy-start | bytes 3076
  212.1 64.8 %all-to-all-start.1 = ((bf16[8,80,2048]{2,1,0:T(8,128)(2,1)}), bf16[8,80,2048]{2,1,0:T(8,128)(2,1)}, u32[]{:S(2)}, u32[]{:S(2)}) async-start(bf16[8,80,2048]{2,1,0:T(8,128)(2,1)} %bitcast.142), calls=%async_computation.1 | async-start | bytes 5242880 | tf_op jit(solution)/shard_map/all_to_all | solution.py:89
  224.9 4.2 %copy-start.1 = (f32[1,128,2048]{2,1,0:T(8,128)S(1)}, f32[1,128,2048]{2,1,0:T(8,128)}, u32[]{:S(2)}) copy-start(f32[1,128,2048]{2,1,0:T(8,128)} %param.14) | copy-start | bytes 3145732
  229.1 47.8 %copy-start.5 = (f32[128,2048]{1,0:T(8,128)}, f32[128,2048]{1,0:T(8,128)S(1)}, u32[]{:S(2)}) copy-start(f32[128,2048]{1,0:T(8,128)S(1)} %reduce_sum.102) | copy-start | bytes 3145732
  286.5 5.0 %copy-start.4 = (f32[1,128,2048]{2,1,0:T(8,128)S(1)}, f32[1,128,2048]{2,1,0:T(8,128)}, u32[]{:S(2)}) copy-start(f32[1,128,2048]{2,1,0:T(8,128)} %param.13) | copy-start | bytes 3145732
  286.5 8.6 %copy-start.2 = (f32[1,128,2048]{2,1,0:T(8,128)S(1)}, f32[1,128,2048]{2,1,0:T(8,128)}, u32[]{:S(2)}) copy-start(f32[1,128,2048]{2,1,0:T(8,128)} %param.14) | copy-start | bytes 3145732
  286.5 8.6 %copy-start.6 = (f32[128,2048]{1,0:T(8,128)S(1)}, f32[128,2048]{1,0:T(8,128)}, u32[]{:S(2)}) copy-start(f32[128,2048]{1,0:T(8,128)} %copy-done.5) | copy-start | bytes 3145732
  286.5 8.6 %copy-start.8 = (bf16[1,128,2048]{2,1,0:T(8,128)(2,1)S(1)}, bf16[1,128,2048]{2,1,0:T(8,128)(2,1)}, u32[]{:S(2)}) copy-start(bf16[1,128,2048]{2,1,0:T(8,128)(2,1)} %param.15) | copy-start | bytes 1572868
  291.7 38.7 %collective-permute-start.1 = (f32[1,128,2048]{2,1,0:T(8,128)S(1)}, f32[1,128,2048]{2,1,0:T(8,128)S(1)}, u32[]{:S(2)}, u32[]{:S(2)}) collective-permute-start(f32[1,128,2048]{2,1,0:T(8,128)S(1)} %fusion.44), channel_id=1, source_target_pairs={{0,8},{8,16},{16,24},{1,9},{9,17},{17,25},{2,10},{10,18},{18,26},{... | collective-permute-start | bytes 3145736 | tf_op jit(solution)/shard_map/ppermute | solution.py:16
  295.8 34.5 %collective-permute-start.4 = (bf16[1,128,2048]{2,1,0:T(8,128)(2,1)S(1)}, bf16[1,128,2048]{2,1,0:T(8,128)(2,1)S(1)}, u32[]{:S(2)}, u32[]{:S(2)}) collective-permute-start(bf16[1,128,2048]{2,1,0:T(8,128)(2,1)S(1)} %fusion.39), channel_id=1, source_target_pairs={{8,0},{16,8},{24,16},{9,1},{17,9},{25,17},{10,2},{18,10},{26,18},{... | collective-permute-start | bytes 1572872 | tf_op jit(solution)/shard_map/ppermute | solution.py:16
where the time goes:
time: 333 us; the launch traced here: 332 us
  waiting for transfers between devices  210 us (63%)
  other arithmetic  35.6 us (11%)
  matrix products  35.6 us (11%)
  starting transfers between devices  27.4 us (8%)
  local copies, waits for them, and re-layouts  22.5 us (7%)
    all_to_all x1, waiting for transfers between devices, backward_experts(): lax.all_to_all(partial_value, 'expert', split_axis=0, concat_axis=0, tile...  48.5 us
    all_to_all x1, waiting for transfers between devices, forward_experts(): lax.all_to_all(partial_value, 'expert', split_axis=0, concat_axis=0, tile...  47.5 us
    ppermute x2, waiting for transfers between devices, from_behind(): lax.ppermute(value, axis, [(source, source + steps) for source in range(l...  33.2 us
    all_to_all x1, waiting for transfers between devices, backward_experts(): lax.all_to_all(send_rows.reshape(units, half_slots, width), 'expert', spl...  31.3 us
    all_to_all x1, waiting for transfers between devices, backward_experts(): lax.all_to_all(send_grads.reshape(units, half_slots, width), 'expert', sp...  26.6 us
    all_to_all x1, waiting for transfers between devices, forward_experts(): lax.all_to_all(send.reshape(units, half_slots, width), 'expert', split_ax...  22.8 us
    dot_general x1, matrix products, expert_backward(): jnp.einsum('rf,df->rd', pre_grad, up_block, preferred_element_type=jnp.fl...  13.1 us
    dot_general x1, matrix products, expert_forward(): jnp.dot(activation, down_block, preferred_element_type=jnp.float32)  11.7 us
  transfers between devices with their start and end apart: 10, of which 6 were waited for; matrix products, arithmetic and copies ran while one was open for 15% of the time, Pallas kernels for 0%

commit v1 on v0

v1 whole, which is shorter than its diff:
```python
import functools

import jax
import jax.numpy as jnp
from jax import lax
from jax.experimental import pallas as pl
from jax.experimental.pallas import tpu as pltpu
from jax.sharding import PartitionSpec as P

norm_eps = 1e-06
F32, BF16 = jnp.float32, jnp.bfloat16
MESH = pl.DeviceIdType.MESH
ROOT, CUBE = 0.7978845608028654, 0.044715


def flip(index, mask, bits):
    total = 0
    for b in range(bits):
        bit = (index // (1 << b)) % 2
        total = total + (1 << b) * (1 - bit if mask >> b & 1 else bit)
    return total


def dot(a, b, ca=1, cb=0):
    return lax.dot_general(a, b, (((ca,), (cb,)), ((), ())), preferred_element_type=F32)


def slot_masks(routes, capacity, slots):
    count = routes.shape[0]
    lanes = lax.broadcasted_iota(jnp.int32, (count, 128), 1)
    hits = [routes[:, k : k + 1] == lanes for k in range(2)]
    choose = jnp.where(hits[0] | hits[1], 1.0, 0.0).astype(BF16)
    row = lax.broadcasted_iota(jnp.int32, (count, count), 0)
    col = lax.broadcasted_iota(jnp.int32, (count, count), 1)
    before = dot(jnp.where(col < row, 1.0, 0.0).astype(BF16), choose)
    places = lax.broadcasted_iota(jnp.int32, (count, slots), 1)
    masks = []
    for k in range(2):
        rank = jnp.sum(jnp.where(hits[k], before, 0.0), axis=1, keepdims=True)
        masks.append(places == routes[:, k : k + 1] * capacity + rank.astype(jnp.int32))
    return masks


def kernel(
    sections, units, capacity,
    x_ref, st_ref, og_ref, fr_ref, fg_ref, fm_ref, br_ref, bg_ref, bm_ref, up_hbm, down_hbm,
    next_ref, grad_ref,
    up, down, snd_f, snd_r, snd_g, rcv_f, rcv_r, rcv_g, act, dgelu,
    px_f, px_b, pin_f, pin_b, ret_f, ret_b, rr_f, rr_b,
    hid, pair0, pair1, normed_b, inv_b, out_f, dh, out_b,
    w_sem, in_send, in_recv, fw_send, fw_recv, px_send, px_recv, rt_send, rt_recv,
    sf_send, sf_recv, sb_send, sb_recv,
):
    s, me = lax.axis_index("section"), lax.axis_index("expert")
    experts = units // 2
    bits = units.bit_length() - 1
    chip, core = me // 2, me % 2
    count, width = x_ref.shape
    half = width // 2
    hidden_units = up.shape[1]
    rows = units * capacity
    slots = experts * capacity
    tile = 256
    group = 16
    order = list(reversed(range(1, units)))
    peer = {k: flip(me, k, bits) for k in order}

    w_up = pltpu.make_async_copy(up_hbm, up, w_sem.at[0])
    w_down = pltpu.make_async_copy(down_hbm, down, w_sem.at[1])
    w_up.start()
    w_down.start()

    barrier = pltpu.get_barrier_semaphore()
    for k in order:
        pl.semaphore_signal(barrier, inc=1, device_id=(s, peer[k]), device_id_type=MESH)
    for step in (1, sections - 1):
        pl.semaphore_signal(
            barrier, inc=1, device_id=((s + step) % sections, me), device_id_type=MESH
        )

    def remote(src, dst, send, recv, section, unit):
        return pltpu.make_async_remote_copy(
            src_ref=src, dst_ref=dst, send_sem=send, recv_sem=recv,
            device_id=(section, unit), device_id_type=MESH,
        )

    def inbound(phase, snd, rcv):
        copies = {}
        for k in order:
            d = peer[k]
            if k == 1:
                src, dst = snd.at[chip], rcv.at[:, me]
            else:
                src, dst = snd.at[d // 2, d % 2], rcv.at[d % 2, me]
            copies[k] = remote(src, dst, in_send.at[phase, k], in_recv.at[phase, k], s, d)
        return copies

    def hand_on(phase, rcv):
        copies = {}
        for k in order:
            if k > 1:
                block = rcv.at[core, peer[k]]
                copies[k] = remote(
                    block, block, fw_send.at[phase, k], fw_recv.at[phase, k], s, peer[1]
                )
        return copies

    def keep_own(snd, rcv):
        for h in range(2):
            rcv[h, me] = snd[chip, h]

    def receive(ins, fws):
        for k in order:
            ins[k].wait_recv()
            if k > 1:
                fws[k].start()
        for k in order:
            if k > 1:
                fws[k].wait_recv()

    def normalise(src, mod, keep):
        @pl.loop(0, count // group)
        def _(i):
            at = pl.ds(pl.multiple_of(i * group, group), group)
            x = src[at, :]
            centered = x - jnp.mean(x, axis=1, keepdims=True)
            inv = lax.rsqrt(jnp.mean(centered * centered, axis=1, keepdims=True) + norm_eps)
            normed = centered * inv
            hid[at, :] = (normed * (1.0 + mod[1:2, :]) + mod[0:1, :]).astype(BF16)
            if keep:
                normed_b[at, :] = normed
                inv_b[at, :] = jnp.broadcast_to(inv, (group, 128))

    def pack(terms, snd):
        for h in range(2):
            @pl.loop(0, half // tile)
            def _(n):
                src = pl.ds(pl.multiple_of(h * half + n * tile, tile), tile)
                value = sum(dot(mask, ref[:, src], 0, 0) for mask, ref in terms).astype(BF16)
                for e in range(experts):
                    snd[e, h, :, pl.ds(pl.multiple_of(n * tile, tile), tile)] = value[
                        e * capacity : (e + 1) * capacity, :
                    ]

    def onehot(mask):
        return jnp.where(mask, 1.0, 0.0).astype(BF16)

    normalise(x_ref, fm_ref, False)
    fwd = slot_masks(fr_ref[...], capacity, slots)
    pack([(onehot(fwd[0] | fwd[1]), hid)], snd_f)
    pl.semaphore_wait(barrier, units + 1)
    in_f, fw_f = inbound(0, snd_f, rcv_f), hand_on(0, rcv_f)
    for k in order:
        in_f[k].start()
    keep_own(snd_f, rcv_f)

    normalise(st_ref, bm_ref, True)
    bwd = slot_masks(br_ref[...], capacity, slots)
    bwd_hot = [onehot(mask) for mask in bwd]
    pack([(bwd_hot[0] + bwd_hot[1], hid)], snd_r)
    in_r, fw_r = inbound(1, snd_r, rcv_r), hand_on(1, rcv_r)
    for k in order:
        in_r[k].start()
    keep_own(snd_r, rcv_r)

    @pl.loop(0, count // group)
    def _(i):
        at = pl.ds(pl.multiple_of(i * group, group), group)
        scaled = bm_ref[2:3, :] * og_ref[at, :].astype(F32)
        pair0[at, :] = (bg_ref[at, 0:1] * scaled).astype(BF16)
        pair1[at, :] = (bg_ref[at, 1:2] * scaled).astype(BF16)

    pack([(bwd_hot[0], pair0), (bwd_hot[1], pair1)], snd_g)
    in_g, fw_g = inbound(2, snd_g, rcv_g), hand_on(2, rcv_g)
    for k in order:
        in_g[k].start()
    keep_own(snd_g, rcv_g)

    def flat(ref, h):
        return ref[h].reshape(rows, half)

    def cols(n, base=0):
        return pl.ds(pl.multiple_of(base + n * tile, tile), tile)

    def exchange(phase, px, pin, ret, result):
        def fill(dst, h):
            @pl.loop(0, half // tile)
            def _(n):
                value = result(h, n).astype(BF16).reshape(units, capacity, tile)
                dst[:, :, cols(n)] = value

        fill(px, 1 - core)
        swap = remote(px, pin, px_send.at[phase], px_recv.at[phase], s, peer[1])
        swap.start()
        fill(ret, core)
        swap.wait_recv()

        @pl.loop(0, units)
        def _(u):
            ret[u] = (ret[u].astype(F32) + pin[u].astype(F32)).astype(BF16)

        return swap

    def give_back(phase, ret, rr):
        copies = {}
        for k in order:
            copies[k] = remote(
                ret.at[peer[k]], rr.at[core, chip],
                rt_send.at[phase, k], rt_recv.at[phase, k], s, peer[k],
            )
            copies[k].start()
        rr[core, chip] = ret[me]
        return copies

    receive(in_f, fw_f)
    w_up.wait()
    w_down.wait()

    @pl.loop(0, hidden_units // tile)
    def _(n):
        pre = dot(flat(rcv_f, 0), up[:half, cols(n)]) + dot(flat(rcv_f, 1), up[half:, cols(n)])
        t = jnp.tanh(ROOT * (pre + CUBE * pre * pre * pre))
        act[:, cols(n)] = (0.5 * pre * (1.0 + t)).astype(BF16)

    swap_f = exchange(
        0, px_f, pin_f, ret_f, lambda h, n: dot(act[...], down[:, cols(n, h * half)])
    )
    back_f = give_back(0, ret_f, rr_f)

    receive(in_r, fw_r)

    @pl.loop(0, hidden_units // tile)
    def _(n):
        pre = dot(flat(rcv_r, 0), up[:half, cols(n)]) + dot(flat(rcv_r, 1), up[half:, cols(n)])
        t = jnp.tanh(ROOT * (pre + CUBE * pre * pre * pre))
        slope = ROOT * (1.0 + 3.0 * CUBE * pre * pre)
        dgelu[:, cols(n)] = 0.5 * (1.0 + t) + 0.5 * pre * (1.0 - t * t) * slope

    receive(in_g, fw_g)

    @pl.loop(0, hidden_units // tile)
    def _(n):
        back = dot(flat(rcv_g, 0), down[cols(n), :half], 1, 1) + dot(
            flat(rcv_g, 1), down[cols(n), half:], 1, 1
        )
        act[:, cols(n)] = (back * dgelu[:, cols(n)]).astype(BF16)

    swap_b = exchange(
        1, px_b, pin_b, ret_b, lambda h, n: dot(act[...], up[cols(n, h * half), :], 1, 1)
    )
    back_b = give_back(1, ret_b, rr_b)

    weight = sum(jnp.where(fwd[k], fg_ref[:, k : k + 1], 0.0) for k in range(2))
    high = weight.astype(BF16)
    low = (weight - high.astype(F32)).astype(BF16)
    for k in order:
        back_f[k].wait_recv()
    sends_f = []
    for h in range(2):
        side = pl.ds(h * half, half)

        @pl.loop(0, half // tile)
        def _(n):
            got = rr_f[h, :, :, cols(n)].reshape(slots, tile)
            moe = dot(high, got) + dot(low, got)
            at = cols(n, h * half)
            out_f[:, at] = x_ref[:, at] + fm_ref[2:3, at] * moe

        copy = remote(
            out_f.at[:, side], next_ref.at[:, side], sf_send.at[h], sf_recv.at[h],
            (s + 1) % sections, me,
        )
        sends_f.append(copy)

        @pl.when(s < sections - 1)
        def _():
            copy.start()

    @pl.when(s == 0)
    def _():
        next_ref[...] = jnp.zeros_like(next_ref)

    @pl.when(s == sections - 1)
    def _():
        grad_ref[...] = jnp.zeros_like(grad_ref)

    for k in order:
        back_b[k].wait_recv()
    both = bwd_hot[0] + bwd_hot[1]
    for h in range(2):
        @pl.loop(0, half // tile)
        def _(n):
            got = rr_b[h, :, :, cols(n)].reshape(slots, tile)
            dh[:, cols(n, h * half)] = dot(both, got)

    pieces = 4
    part = count // pieces
    sends_b = []
    for p in range(pieces):
        @pl.loop(0, part // group)
        def _(i):
            at = pl.ds(pl.multiple_of(p * part + i * group, group), group)
            dnorm = dh[at, :] * (1.0 + bm_ref[1:2, :])
            normed = normed_b[at, :]
            one = jnp.mean(dnorm, axis=1, keepdims=True)
            two = jnp.mean(dnorm * normed, axis=1, keepdims=True)
            out_b[at, :] = (
                og_ref[at, :].astype(F32) + (dnorm - one - normed * two) * inv_b[at, 0:1]
            ).astype(BF16)

        piece = pl.ds(p * part, part)
        copy = remote(
            out_b.at[piece], grad_ref.at[piece], sb_send.at[p], sb_recv.at[p],
            (s + sections - 1) % sections, me,
        )
        sends_b.append(copy)

        @pl.when(s > 0)
        def _():
            copy.start()

    for copies in (in_f, in_r, in_g, fw_f, fw_r, fw_g, back_f, back_b):
        for copy in copies.values():
            copy.wait_send()
    swap_f.wait_send()
    swap_b.wait_send()

    @pl.when(s < sections - 1)
    def _():
        for copy in sends_f:
            copy.wait_send()
        for copy in sends_b:
            copy.wait_recv()

    @pl.when(s > 0)
    def _():
        for copy in sends_f:
            copy.wait_recv()
        for copy in sends_b:
            copy.wait_send()


def on_device(
    section_inputs,
    stored_inputs,
    out_grads,
    fwd_routes,
    fwd_gates,
    fwd_modulation,
    bwd_routes,
    bwd_gates,
    bwd_modulation,
    up_weight,
    down_weight,
):
    sections, units = lax.axis_size("section"), lax.axis_size("expert")
    experts = units // 2
    count, width = section_inputs.shape[1:]
    hidden_units = up_weight.shape[3]
    half = width // 2
    capacity = -(-min(count, 5 * count // (2 * experts)) // 16) * 16
    rows = units * capacity

    def vmem(dtype, *shape):
        return pltpu.VMEM(shape, dtype)

    def dma(*shape):
        return pltpu.SemaphoreType.DMA(shape)

    scratch = [
        vmem(BF16, width, hidden_units),
        vmem(BF16, hidden_units, width),
        *[vmem(BF16, experts, 2, capacity, half)] * 3,
        *[vmem(BF16, 2, units, capacity, half)] * 3,
        vmem(BF16, rows, hidden_units),
        vmem(F32, rows, hidden_units),
        *[vmem(BF16, units, capacity, half)] * 6,
        *[vmem(BF16, 2, experts, capacity, half)] * 2,
        *[vmem(BF16, count, width)] * 3,
        vmem(F32, count, width),
        vmem(F32, count, 128),
        *[vmem(F32, count, width)] * 2,
        vmem(BF16, count, width),
        dma(2),
        *[dma(3, units)] * 4,
        *[dma(2)] * 2,
        *[dma(2, units)] * 2,
        *[dma(2)] * 2,
        *[dma(4)] * 2,
    ]
    in_vmem = pl.BlockSpec(memory_space=pltpu.VMEM)
    in_hbm = pl.BlockSpec(memory_space=pl.ANY)
    flops = 10 * rows * width * hidden_units
    next_inputs, input_grads = pl.pallas_call(
        functools.partial(kernel, sections, units, capacity),
        out_shape=(
            jax.ShapeDtypeStruct((count, width), F32),
            jax.ShapeDtypeStruct((count, width), BF16),
        ),
        in_specs=[in_vmem] * 9 + [in_hbm] * 2,
        out_specs=(in_vmem, in_vmem),
        scratch_shapes=scratch,
        compiler_params=pltpu.CompilerParams(
            collective_id=0, has_side_effects=True, vmem_limit_bytes=67043328
        ),
        cost_estimate=pl.CostEstimate(
            flops=flops, bytes_accessed=4 * width * hidden_units, transcendentals=0
        ),
    )(
        section_inputs[0], stored_inputs[0], out_grads[0], fwd_routes[0], fwd_gates[0],
        fwd_modulation[0], bwd_routes[0], bwd_gates[0], bwd_modulation[0],
        up_weight[0, 0], down_weight[0, 0],
    )
    return next_inputs[None], input_grads[None]


def solution(mesh):
    tokens = P("section", "expert", None)
    shared = P("section", None, None)
    weights = P("section", "expert", None, None)
    placed = (tokens,) * 5 + (shared,) + (tokens,) * 2 + (shared,) + (weights,) * 2
    return jax.shard_map(
        on_device,
        mesh=mesh,
        in_specs=placed,
        out_specs=(tokens, tokens),
        check_vma=False,
    )
```

time: 333 us -> 188 us (0.56)
  waiting for transfers between devices: 210 us -> 0 us
  Pallas kernels: 0 us -> 175 us
  matrix products: 35.6 us -> 0 us
  other arithmetic: 35.6 us -> 0 us
  starting transfers between devices: 27.4 us -> 0 us
  local copies, waits for them, and re-layouts: 22.5 us -> 11.2 us
    all_to_all x5 -> x0, waiting for transfers between devices: 177 us -> none  [the longest x1 48.5 us: backward_experts(): lax.all_to_all(partial_value, 'expert', split_axis=0, concat_axis=0, tile...]
    pallas_call x0 -> x1, Pallas kernels: none -> 175 us  [on_device(): pl.pallas_call(functools.partial(kernel, sections, units, capacity), out_...]
    dot_general x6 -> x0, matrix products: 35.6 us -> none  [the longest x1 13.1 us: expert_backward(): jnp.einsum('rf,df->rd', pre_grad, up_block, preferred_element_type=jnp.fl...]
    ppermute x5 -> x0, waiting for transfers between devices: 33.2 us -> none  [the longest x2 33.2 us: from_behind(): lax.ppermute(value, axis, [(source, source + steps) for source in range(l...]
    all_to_all x5 -> x0, starting transfers between devices: 22 us -> none  [the longest x1 6.35 us: forward_experts(): lax.all_to_all(send.reshape(units, half_slots, width), 'expert', split_ax...]
    select_n x6 -> x0, other arithmetic: 14.1 us -> none  [the longest x2 10.5 us: join_partner(): return jnp.where(parity == 0, first, second)]
    reduce_sum x9 -> x0, other arithmetic: 12.8 us -> none  [the longest x1 4.97 us: on_device(): moe_out = jnp.sum(pair_out * fwd_gates[0][:, :, None], axis=1)]
    unnamed x33 -> x7, local copies, waits for them, and re-layouts: 2.93 us -> 11.2 us
  transfers between devices with their start and end apart: 10 -> 0, of which waited for: 6 -> 0; matrix products, arithmetic and copies ran while one was open for 15% -> 0% of each run, Pallas kernels for 0% -> 0%
where the time goes in v1:
time: 188 us; the launch traced here: 187 us
  Pallas kernels  175 us (93%)
  local copies, waits for them, and re-layouts  11.2 us (6%)
    pallas_call x1, Pallas kernels, on_device(): pl.pallas_call(functools.partial(kernel, sections, units, capacity), out_...  175 us
    unnamed x7, local copies, waits for them, and re-layouts  11.2 us

profile of v1, /device:TPU:0, one launch (start us, length us, event | category | flops | bytes accessed | tf_op | source)
XLA Modules:
  0.0 187.3 jit_solution(16943553836044083018)
XLA Ops:
  0.6 1.4 copy.13
  2.0 1.4 copy.14
  3.5 1.4 copy.15
  4.9 1.4 copy.16
  6.3 1.4 copy_bitcast_fusion
  7.6 175.5 %shard_map.122 = (f32[128,2048]{1,0:T(8,128)}, bf16[128,2048]{1,0:T(8,128)(2,1)}) custom-call(f32[128,2048]{1,0:T(8,128)} %bitcast.23, f32[128,2048]{1,0:T(8,128)} %bitcast.24, bf16[128,2048]{1,0:T(8,128)(2,1)} %bitcast.25, s32[128,2]{1,0:T(8,128)} %bitcast.17, f32[128,2]{1,0:T(8,128)} %bitcast.18, f32[3,2048]{1,0:T(4,128)} %get-tuple-element.7.fm_ref, ...), custom_call_target="tpu_custom_call" | custom-call | flops 13421772800 | bytes 8388608 | tf_op jit(solution)/shard_map/pallas_call | solution.py:394
  183.2 2.3 %copy.23 = f32[1,128,2048]{2,1,0:T(8,128)} copy(f32[1,128,2048]{2,1,0:T(8,128)} %bitcast.15) | data formatting | bytes 2097152
  185.5 1.9 %copy.24 = bf16[1,128,2048]{2,1,0:T(8,128)(2,1)} copy(bf16[1,128,2048]{2,1,0:T(8,128)(2,1)} %bitcast.16) | data formatting | bytes 1048576

commit v2 on v1

--- a/solution.py
+++ b/solution.py
@@ -62,7 +62,7 @@
     slots = experts * capacity
     tile = 256
     group = 16
-    order = list(reversed(range(1, units)))
+    order = list(range(1, units))
     peer = {k: flip(me, k, bits) for k in order}
 
     w_up = pltpu.make_async_copy(up_hbm, up, w_sem.at[0])

time: 188 us -> 179 us (0.952)
  the two profiles are of different devices: /device:TPU:0 before, /device:TPU:11 now
where the time goes in v2:
time: 179 us; the launch traced here: 178 us
  Pallas kernels  166 us (93%)
  local copies, waits for them, and re-layouts  11.2 us (6%)
    pallas_call x1, Pallas kernels, on_device(): pl.pallas_call(functools.partial(kernel, sections, units, capacity), out_...  166 us
    unnamed x7, local copies, waits for them, and re-layouts  11.2 us

profile of v2, /device:TPU:11, one launch (start us, length us, event | category | flops | bytes accessed | tf_op | source)
XLA Modules:
  0.0 178.3 jit_solution(10593744077870555965)
XLA Ops:
  0.6 1.4 copy.13
  2.0 1.4 copy.14
  3.5 1.4 copy.15
  4.9 1.4 copy.16
  6.3 1.4 copy_bitcast_fusion
  7.6 166.4 %shard_map.122 = (f32[128,2048]{1,0:T(8,128)}, bf16[128,2048]{1,0:T(8,128)(2,1)}) custom-call(f32[128,2048]{1,0:T(8,128)} %bitcast.23, f32[128,2048]{1,0:T(8,128)} %bitcast.24, bf16[128,2048]{1,0:T(8,128)(2,1)} %bitcast.25, s32[128,2]{1,0:T(8,128)} %bitcast.17, f32[128,2]{1,0:T(8,128)} %bitcast.18, f32[3,2048]{1,0:T(4,128)} %get-tuple-element.7.fm_ref, ...), custom_call_target="tpu_custom_call" | custom-call | flops 13421772800 | bytes 8388608 | tf_op jit(solution)/shard_map/pallas_call | solution.py:394
  174.1 2.3 %copy.23 = f32[1,128,2048]{2,1,0:T(8,128)} copy(f32[1,128,2048]{2,1,0:T(8,128)} %bitcast.15) | data formatting | bytes 2097152
  176.4 1.9 %copy.24 = bf16[1,128,2048]{2,1,0:T(8,128)(2,1)} copy(bf16[1,128,2048]{2,1,0:T(8,128)(2,1)} %bitcast.16) | data formatting | bytes 1048576
